TPU v7x, 32 devices: a whole 2x2x4 slice. The times are simulated.
32 devices in a mesh: gx: 4 (over z), gy: 8 (over y, x, core).
Axes of the slice: x: 2, y: 2, z: 4, core: 2. Of those that a mesh axis runs over, the one named last changes fastest.
Arguments:
- right_side: float32 [512, 2048], P('gx', 'gy'), may hold values from -1.2 to 1.2
- shift: float32 [512, 2048], P('gx', 'gy'), may hold values from 0.0001 to 0.004
Outputs:
- solution: float32 [512, 2048], P('gx', 'gy')
- residual: float32 [512, 2048], P('gx', 'gy')
All inputs are finite; a program needn't handle non-finite values.
Results may differ from a plain program's by a relative error of at most 0.0003.
Values sent between devices are 32-bit elements; how exact they have to be, the bound alone decides.
A program may use at most 128 MiB of HBM per device.

v0:
```python
import functools

import jax
import jax.numpy as jnp
from jax import lax
from jax.experimental import pallas as pl
from jax.experimental.pallas import tpu as pltpu
from jax.sharding import PartitionSpec as P

COARSE_SWEEPS = 6
DAMPING = 0.8
MESH = pl.DeviceIdType.MESH
F32 = jnp.float32
BF16 = jnp.bfloat16

ROWS_PAD = 8
HALO = 8
ROW_HALO = 32


def iota(shape, dim):
    return lax.broadcasted_iota(jnp.int32, shape, dim)


def put_strips(ref, at, values):
    for k in range(ref.shape[0]):
        ref[k, at, :] = values[:, k * 128 : (k + 1) * 128]


def get_strips(ref, at, count=None):
    return jnp.concatenate([ref[k, at, :] for k in range(count or ref.shape[0])], 1)


def exact_dot(values, selector):
    first = values.astype(BF16)
    rest = values - first.astype(F32)
    second = rest.astype(BF16)
    third = (rest - second.astype(F32)).astype(BF16)
    dot = functools.partial(jnp.dot, preferred_element_type=F32)
    return dot(first, selector) + (dot(second, selector) + dot(third, selector))


def kernel(
    gx_count, gy_count, g_hbm, s_hbm, out_ref,
    g_ref, s_ref, load_sem,
    gE, sE, wE, vA, vB, fine_add,
    gP, sP, wP, aP, bP,
    g1, s1, w1, a1, b1, r1,
    send_l, send_r, recv_l, recv_r,
    down0, up0, down1, spread, down_w, up_w,
    rbuf, cbuf, s2, w2, g2, a2, b2, s3, w3, g3, a3, b3, s4, w4, g4, a4, b4, picked,
    s2w, w2w, s3w, w3w,
    halo_send, halo_recv, row_send, row_recv, all_send, all_recv, coarse_sems,
):
    gx, gy = lax.axis_index("gx"), lax.axis_index("gy")
    total = gx_count * gy_count
    me = gx * gy_count + gy
    rows, cols = g_hbm.shape
    base = ROWS_PAD + HALO
    base1 = ROWS_PAD + (ROWS_PAD + HALO) // 2
    ext, width = gE.shape
    ext1, width1 = ext // 2, g1.shape[1]
    half_rows = rows // 2
    base_w = ROWS_PAD + ROW_HALO
    near1 = slice(ROWS_PAD, ROWS_PAD + ext1)
    wide1 = slice(ROWS_PAD, base_w + half_rows + ROW_HALO)
    lanes = 128

    load_g = pltpu.make_async_copy(g_hbm, g_ref, load_sem.at[0])
    load_s = pltpu.make_async_copy(s_hbm, s_ref, load_sem.at[1])
    load_g.start()
    load_s.start()
    zero_halo = jnp.zeros((base, width), F32)
    for ref in (gE, sE):
        ref[0:base, :] = zero_halo
        ref[base + rows : ext, :] = zero_halo
    for ref in (recv_l, recv_r):
        ref[...] = jnp.zeros(ref.shape, F32)
    for ref in (g1, s1):
        ref[0:base_w, :] = jnp.zeros((base_w, width1), F32)
        ref[base_w + half_rows :, :] = jnp.zeros((base_w, width1), F32)
    barrier = pltpu.get_barrier_semaphore()

    @pl.loop(1, total)
    def _(k):
        peer = lax.rem(me + k, total)
        pl.semaphore_signal(
            barrier, inc=1, device_id=(peer // gy_count, lax.rem(peer, gy_count)), device_id_type=MESH
        )

    lane = iota((rows, lanes), 1)
    half = lanes // 2
    l0 = iota((width, width1), 0)
    col0 = jnp.where(l0 < cols + half, l0, l0 - width)
    down0[...] = jnp.where(
        ((col0 + 2 * width1) // 2) % width1 == iota((width, width1), 1), 1.0, 0.0
    ).astype(BF16)
    l0 = iota((width1, width), 1)
    col0 = jnp.where(l0 < cols + half, l0, l0 - width)
    up0[...] = jnp.where(
        ((col0 + 2 * width1) // 2) % width1 == iota((width1, width), 0), 1.0, 0.0
    ).astype(BF16)
    l1 = iota((width1, lanes), 0)
    j2 = l1 // 2
    place = (j2 % 4) * 16 + j2 // 4
    down1[...] = jnp.where(
        (l1 < lanes) & (iota((width1, lanes), 1) % half == place), 1.0, 0.0
    ).astype(BF16)
    q_count = s2.shape[2]
    p_count = s2.shape[1]
    m1 = iota((q_count, width1), 1)
    col1 = jnp.where(m1 < lanes + half // 2, m1, m1 - width1)
    wide = gy * half + (col1 + 512) // 2 - 256
    for r in range(4):
        spread[r * q_count : (r + 1) * q_count, :] = jnp.where(
            wide == 4 * iota((q_count, width1), 0) + r, 1.0, 0.0
        ).astype(BF16)

    load_g.wait()
    load_s.wait()
    send_l[...] = jnp.where(lane < half, g_ref[:, 0:lanes], pltpu.roll(s_ref[:, 0:lanes], half, 1))
    send_r[...] = jnp.where(
        lane < half, pltpu.roll(s_ref[:, cols - lanes : cols], half, 1), g_ref[:, cols - lanes : cols]
    )

    l1 = iota((width1, lanes), 0)
    at2 = (jnp.where(l1 < lanes + half // 2, l1, l1 - width1) + 2 * lanes) // 2
    at4 = at2 // 4 - 24
    down_w[...] = jnp.where(
        (at4 >= 0) & (at4 < 32) & (iota((width1, lanes), 1) == (at2 % 4) * 32 + at4), 1.0, 0.0
    ).astype(BF16)
    l1 = iota((lanes, width1), 1)
    at2 = (jnp.where(l1 < lanes + half // 2, l1, l1 - width1) + 2 * lanes) // 2
    at4 = at2 // 4 - 24
    up_w[...] = jnp.where(
        (at4 >= 0) & (at4 < 32) & (iota((lanes, width1), 0) == (at2 % 4) * 32 + at4), 1.0, 0.0
    ).astype(BF16)

    def pack_level2(source):
        parts = []
        for t in range(4):
            start = base1 + 2 * t
            parts.append(
                get_strips(source, pl.ds(start, 8, 8)) + get_strips(source, pl.ds(start + 1, 8, 8))
            )
        means = 0.25 * exact_dot(jnp.concatenate(parts, 0), down1[...])
        low = iota((16, lanes), 1) < half
        return jnp.where(low, means[0:16], means[16:32])

    own_strips = cols // lanes
    for k in range(own_strips):
        fine_add[k, base : base + rows, :] = s_ref[:, k * lanes : (k + 1) * lanes]
    own = get_strips(fine_add, pl.ds(base, half_rows, 2), own_strips)
    own = own + get_strips(fine_add, pl.ds(base + 1, half_rows, 2), own_strips)
    put_strips(r1, slice(base1, base1 + half_rows), 0.25 * exact_dot(own, down0[0:cols, :]))
    rbuf[0, me] = pack_level2(r1)
    gE[base : base + rows, 0:cols] = g_ref[...]
    sE[base : base + rows, 0:cols] = s_ref[...]

    pl.semaphore_wait(barrier, total - 1)

    top, bottom = slice(0, HALO), slice(rows - HALO, rows)
    above, below = slice(ROWS_PAD, base), slice(base + rows, base + rows + HALO)
    middle = slice(base, base + rows)
    sends = (
        (0, -1, send_l, recv_r.at[middle, :]),
        (0, 1, send_r, recv_l.at[middle, :]),
        (-1, -1, send_l.at[top, :], recv_r.at[below, :]),
        (1, -1, send_l.at[bottom, :], recv_r.at[above, :]),
        (-1, 1, send_r.at[top, :], recv_l.at[below, :]),
        (1, 1, send_r.at[bottom, :], recv_l.at[above, :]),
        (-1, 0, g_ref.at[top, :], gE.at[below, 0:cols]),
        (-1, 0, s_ref.at[top, :], sE.at[below, 0:cols]),
        (1, 0, g_ref.at[bottom, :], gE.at[above, 0:cols]),
        (1, 0, s_ref.at[bottom, :], sE.at[above, 0:cols]),
    )

    def inside(dx, dy):
        ok = None
        for step, at, count in ((dx, gx, gx_count), (dy, gy, gy_count)):
            if step:
                here = (at > 0) if step < 0 else (at < count - 1)
                ok = here if ok is None else ok & here
        return ok

    def halo_copy(n, dx, dy, source, target):
        return pltpu.make_async_remote_copy(
            src_ref=source, dst_ref=target, send_sem=halo_send.at[n], recv_sem=halo_recv.at[n],
            device_id=(gx + dx, gy + dy), device_id_type=MESH,
        )

    for n, (dx, dy, source, target) in enumerate(sends):
        @pl.when(inside(dx, dy))
        def _():
            halo_copy(n, dx, dy, source, target).start()

    core = lax.rem(gy, 2)
    per_row = gy_count // 2
    chips = total // 2
    chip = me // 2
    partner = (gx, gy + 1 - 2 * core)

    def zigzag(j):
        odd = lax.rem(j, 2)
        return odd * ((j + 1) // 2) + (1 - odd) * (chips - j // 2)

    def block_copy(turn, n, slot, peer):
        return pltpu.make_async_remote_copy(
            src_ref=rbuf.at[turn, slot], dst_ref=rbuf.at[turn, slot],
            send_sem=all_send.at[turn, n], recv_sem=all_recv.at[turn, slot],
            device_id=peer, device_id_type=MESH,
        )

    def direct(turn, j):
        other = lax.rem(chip + zigzag(j), chips)
        return block_copy(turn, j, me, (other // per_row, 2 * lax.rem(other, per_row) + core))

    def onward(turn, j):
        slot = 2 * lax.rem(chip + chips - zigzag(j), chips) + core
        return block_copy(turn, chips + j, slot, partner)

    def gather_start(turn):
        block_copy(turn, 0, me, partner).start()

        @pl.loop(1, chips)
        def _(j):
            direct(turn, chips - j).start()

    def gather_wait(turn):
        @pl.loop(1, chips)
        def _(j):
            copy = onward(turn, j)
            copy.wait_recv()
            copy.start()

        block_copy(turn, 0, me + 1 - 2 * core, partner).wait_recv()

        @pl.loop(1, chips)
        def _(j):
            slot = 2 * lax.rem(chip + chips - zigzag(j), chips) + 1 - core
            block_copy(turn, chips + j, slot, partner).wait_recv()

    def gather_sent(turn):
        block_copy(turn, 0, me, partner).wait_send()

        @pl.loop(1, chips)
        def _(j):
            direct(turn, j).wait_send()
            onward(turn, j).wait_send()

    gather_start(0)
    zero_tile = jnp.zeros((ROWS_PAD, width), F32)
    for ref in (vA, vB):
        ref[0:ROWS_PAD, :] = zero_tile
        ref[ext - ROWS_PAD : ext, :] = zero_tile
    for ref in (aP, bP, a1, b1):
        ref[0:ROWS_PAD, :] = jnp.zeros((ROWS_PAD, width1), F32)
        ref[ref.shape[0] - ROWS_PAD :, :] = jnp.zeros((ROWS_PAD, width1), F32)
    for ref in (a2, b2, a3, b3, a4, b4):
        for i in range(ref.shape[0]):
            ref[i, 0:8, :] = jnp.zeros((8, q_count), F32)
            ref[i, 8 + p_count : 16 + p_count, :] = jnp.zeros((8, q_count), F32)

    for n, (dx, dy, source, target) in enumerate(sends):
        @pl.when(inside(-dx, -dy))
        def _():
            halo_copy(n, -dx, -dy, source, target).wait_recv()

    lane_e = iota((ext, lanes), 1)
    gE[:, cols:width] = jnp.where(lane_e < half, recv_r[...], recv_l[...])
    sE[:, cols:width] = pltpu.roll(jnp.where(lane_e < half, recv_l[...], recv_r[...]), half, 1)

    def weight(shifts, first_row, own_rows, own_cols, split, level):
        shape = shifts.shape
        at_row = gx * own_rows + iota(shape, 0) + first_row
        lane_at = iota(shape, 1)
        at_col = gy * own_cols + jnp.where(lane_at < own_cols + split, lane_at, lane_at - shape[1])
        good = (at_row >= 0) & (at_row < gx_count * own_rows)
        good = good & (at_col >= 0) & (at_col < gy_count * own_cols)
        return jnp.where(good, DAMPING / (4.0 ** (1 - level) + shifts), 0.0)

    def around(v, lo, size):
        span = v.shape[1]
        mid = v[lo : lo + size, :]
        beside = pltpu.roll(mid, 1, 1) + pltpu.roll(mid, span - 1, 1)
        return mid, beside + (v[lo - 1 : lo - 1 + size, :] + v[lo + 1 : lo + 1 + size, :])

    def sweep_block(v, out, g, w, level, span=None):
        scale = 4.0 ** (-level)
        for lo in range(*(span or (ROWS_PAD, v.shape[0] - ROWS_PAD)), 8):
            mid, beside = around(v, lo, 8)
            at = slice(lo, lo + 8)
            out[at, :] = (1.0 - DAMPING) * mid + w[at, :] * (g[at, :] + scale * beside)

    def residual_block(v, out, g, s, level, span=None):
        scale = 4.0 ** (-level)
        for lo in range(*(span or (ROWS_PAD, v.shape[0] - ROWS_PAD)), 8):
            mid, beside = around(v, lo, 8)
            at = slice(lo, lo + 8)
            put_strips(out, at, g[at, :] - (scale * (4.0 * mid - beside) + s[at, :] * mid))

    row_moves = (
        (-1, sP.at[base1 : base1 + ROW_HALO, :], s1.at[base_w + half_rows : base_w + half_rows + ROW_HALO, :]),
        (1, sP.at[base1 + half_rows - ROW_HALO : base1 + half_rows, :], s1.at[ROWS_PAD:base_w, :]),
        (-1, gP.at[base1 : base1 + ROW_HALO, :], g1.at[base_w + half_rows : base_w + half_rows + ROW_HALO, :]),
        (1, gP.at[base1 + half_rows - ROW_HALO : base1 + half_rows, :], g1.at[ROWS_PAD:base_w, :]),
    )

    def row_copy(n, dx):
        _, source, target = row_moves[n]
        return pltpu.make_async_remote_copy(
            src_ref=source, dst_ref=target, send_sem=row_send.at[n], recv_sem=row_recv.at[n],
            device_id=(gx + dx, gy), device_id_type=MESH,
        )

    def rows_start(which):
        for n in which:
            dx = row_moves[n][0]
            @pl.when(inside(dx, 0))
            def _():
                row_copy(n, dx).start()

    def halved():
        pairs = get_strips(fine_add, pl.ds(0, ext1, 2)) + get_strips(fine_add, pl.ds(1, ext1, 2))
        return 0.25 * exact_dot(pairs, down0[...])

    put_strips(fine_add, slice(0, ext), sE[...])
    sP[near1, :] = halved()
    rows_start((0, 1))
    chunk = 16
    for lo in range(0, ext, chunk):
        at = slice(lo, lo + chunk)
        wE[at, :] = weight(sE[at, :], lo - base, rows, cols, half, 0)
    for lo in range(ROWS_PAD, ext - ROWS_PAD, 8):
        at = slice(lo, lo + 8)
        vA[at, :] = wE[at, :] * gE[at, :]
    sweep_block(vA, vB, gE, wE, 0)
    put_strips(fine_add, slice(0, ROWS_PAD), zero_tile)
    put_strips(fine_add, slice(ext - ROWS_PAD, ext), zero_tile)
    residual_block(vB, fine_add, gE, sE, 0)
    gP[near1, :] = halved()
    wP[near1, :] = weight(sP[near1, :], ROWS_PAD - base1, half_rows, cols // 2, half // 2, 1)
    aP[near1, :] = wP[near1, :] * gP[near1, :]
    sweep_block(aP, bP, gP, wP, 1)
    residual_block(bP, r1, gP, sP, 1, (base1, base1 + half_rows))
    rbuf[1, me] = pack_level2(r1)
    gather_start(1)
    rows_start((2, 3))

    block = (lane_e[0:8] // 16)

    def unpack(turn, target):
        for x in range(gx_count):
            for u in range(gy_count // 8):
                for tl in range(2):
                    tiles = [rbuf[turn, x * gy_count + u * 8 + g, tl * 8 : tl * 8 + 8, :] for g in range(8)]
                    for bit in (1, 2, 4):
                        keep = (block & bit) == 0
                        fresh = list(tiles)
                        for g in range(8):
                            if g & bit == 0:
                                lo, hi = tiles[g], tiles[g | bit]
                                fresh[g] = jnp.where(keep, lo, pltpu.roll(hi, 16 * bit, 1))
                                fresh[g | bit] = jnp.where(keep, pltpu.roll(lo, lanes - 16 * bit, 1), hi)
                        tiles = fresh
                    for b in range(8):
                        t, r = (b // 4) * 2 + tl, b % 4
                        target[t * 4 + r, 8 * x : 8 * x + 8, u * lanes : (u + 1) * lanes] = tiles[b]

    lane_q = iota((p_count, q_count), 1)
    rows_q = slice(8, 8 + p_count)

    def sides(v, n, t, r):
        mid = v[t * n + r, rows_q, :]
        if t > 0:
            north = v[(t - 1) * n + r, rows_q, :]
        else:
            north = v[(n - 1) * n + r, 7 : 7 + p_count, :]
        if t < n - 1:
            south = v[(t + 1) * n + r, rows_q, :]
        else:
            south = v[r, 9 : 9 + p_count, :]
        if r > 0:
            west = v[t * n + r - 1, rows_q, :]
        else:
            west = jnp.where(lane_q == 0, 0.0, pltpu.roll(v[t * n + n - 1, rows_q, :], 1, 1))
        if r < n - 1:
            east = v[t * n + r + 1, rows_q, :]
        else:
            east = jnp.where(
                lane_q == q_count - 1, 0.0, pltpu.roll(v[t * n, rows_q, :], q_count - 1, 1)
            )
        return mid, (north + south) + (west + east)

    level_refs = {2: (s2, w2, g2, a2, b2, 4), 3: (s3, w3, g3, a3, b3, 2), 4: (s4, w4, g4, a4, b4, 1)}

    def sweep(level, v, out):
        s, w, g, _, _, n = level_refs[level]
        for t in range(n):
            for r in range(n):
                i = t * n + r
                mid, beside = sides(v, n, t, r)
                out[i, rows_q, :] = (1.0 - DAMPING) * mid + w[i] * (g[i] + 4.0 ** (-level) * beside)

    def first_sweep(level, out):
        s, w, g, _, _, n = level_refs[level]
        for i in range(n * n):
            out[i, rows_q, :] = w[i] * g[i]

    def restricted(level, v):
        s, w, g, _, _, n = level_refs[level]
        coarse_g = level_refs[level + 1][2]
        for t in range(n // 2):
            for r in range(n // 2):
                sums = None
                for dt in range(2):
                    for dr in range(2):
                        i = (2 * t + dt) * n + 2 * r + dr
                        mid, beside = sides(v, n, 2 * t + dt, 2 * r + dr)
                        left = g[i] - (4.0 ** (-level) * (4.0 * mid - beside) + s[i] * mid)
                        sums = left if sums is None else sums + left
                coarse_g[t * (n // 2) + r] = 0.25 * sums

    def correct(level, v, e):
        n = level_refs[level][5]
        for t in range(n):
            for r in range(n):
                i = t * n + r
                v[i, rows_q, :] = v[i, rows_q, :] + e[(t // 2) * (n // 2) + r // 2, rows_q, :]

    def prepare(level):
        s, w, _, _, _, n = level_refs[level]
        for i in range(n * n):
            w[i] = DAMPING / (4.0 ** (1 - level) + s[i])
        if level < 4:
            coarse_s = level_refs[level + 1][0]
            m = n // 2
            for t in range(m):
                for r in range(m):
                    i = 2 * t * n + 2 * r
                    coarse_s[t * m + r] = 0.25 * ((s[i] + s[i + n]) + (s[i + 1] + s[i + n + 1]))

    def total_of(x):
        return jnp.sum(jnp.sum(x, axis=0, keepdims=True), axis=1, keepdims=True)

    gather_wait(0)
    unpack(0, s2)
    for level in (2, 3, 4):
        prepare(level)
    row_q = iota((p_count, q_count), 0)
    edges = jnp.where(row_q == 0, 1.0, 0.0) + jnp.where(row_q == p_count - 1, 1.0, 0.0)
    edges = edges + jnp.where(lane_q == 0, 1.0, 0.0) + jnp.where(lane_q == q_count - 1, 1.0, 0.0)
    per_unit = 1.0 / total_of(4.0 ** (-4) * edges + s4[0])

    def coarse(v, from_zero):
        if from_zero:
            shifted = jnp.zeros((p_count, q_count), F32) + total_of(g4[0]) * per_unit
        else:
            mid, beside = sides(v, 1, 0, 0)
            left = g4[0] - (4.0 ** (-4) * (4.0 * mid - beside) + s4[0] * mid)
            shifted = mid + total_of(left) * per_unit
        now, later = a4, b4
        now[0, rows_q, :] = shifted
        for _ in range(COARSE_SWEEPS):
            sweep(4, now, later)
            now, later = later, now
        return now

    def vcycle(level, v):
        if level == 4:
            return coarse(v, v is None)
        _, _, _, a, b, n = level_refs[level]
        if v is None:
            first_sweep(level, a)
            sweep(level, a, b)
            now, later = b, a
        else:
            later = b if v is a else a
            sweep(level, v, later)
            sweep(level, later, v)
            now = v
        restricted(level, now)
        correct(level, now, vcycle(level + 1, None))
        sweep(level, now, later)
        sweep(level, later, now)
        return now

    def fcycle(level):
        if level == 4:
            return coarse(None, True)
        _, _, _, a, b, n = level_refs[level]
        first_sweep(level, a)
        sweep(level, a, b)
        restricted(level, b)
        e = fcycle(level + 1)
        e = vcycle(level + 1, e)
        correct(level, b, e)
        sweep(level, b, a)
        sweep(level, a, b)
        return b

    window = picked.shape[1] - 8
    lane_w, row_w = iota((window, lanes), 1), iota((window, lanes), 0)

    def in_domain(period):
        at_p, at_q = gx * 8 - 4 + row_w, gy * 16 - 8 + lane_w % period
        good = (at_p >= 0) & (at_p < p_count) & (at_q >= 0) & (at_q < q_count)
        return good & (lane_w % period < 32)

    def put_window(t, values):
        for a in range(2):
            put_strips(r1, pl.ds(ROWS_PAD + 2 * t + a, window, 8), values)

    def add_level2(e, v):
        for t in range(4):
            tiles = [e[t * 4 + r, pl.ds(pl.multiple_of(gx * 8, 8), 24), :] for r in range(4)]
            picked[t] = exact_dot(jnp.concatenate(tiles, 1), spread[...])
        for t in range(4):
            put_window(t, picked[t, 4 : 4 + window, :])
        v[wide1, :] = v[wide1, :] + get_strips(r1, wide1)

    def pack_window(source):
        parts = []
        for t in range(4):
            start = ROWS_PAD + 2 * t
            parts.append(
                get_strips(source, pl.ds(start, window, 8)) + get_strips(source, pl.ds(start + 1, window, 8))
            )
        means = 0.25 * exact_dot(jnp.concatenate(parts, 0), down_w[...])
        return [means[t * window : (t + 1) * window] for t in range(4)]

    def joined(x, unit):
        return x + pltpu.roll(x, lanes - unit, 1)

    def halved_window(tiles, unit):
        return [0.25 * joined(tiles[2 * t] + tiles[2 * t + 1], unit) for t in range(len(tiles) // 2)]

    def beside_window(v, unit):
        n = len(v)
        out = []
        for t in range(n):
            north = v[t - 1] if t > 0 else pltpu.roll(v[n - 1], 1, 0)
            south = v[t + 1] if t < n - 1 else pltpu.roll(v[0], window - 1, 0)
            west = jnp.where(lane_w < unit, pltpu.roll(v[t], unit + 1, 1), pltpu.roll(v[t], unit, 1))
            east = jnp.where(
                lane_w >= lanes - unit,
                pltpu.roll(v[t], lanes - unit - 1, 1), pltpu.roll(v[t], lanes - unit, 1),
            )
            out.append((north + south) + (west + east))
        return out

    window_refs = {2: (s2w, w2w, 32), 3: (s3w, w3w, 64)}

    def sweep_window(level, v, g):
        _, w, unit = window_refs[level]
        beside = beside_window(v, unit)
        return [
            (1.0 - DAMPING) * v[t] + w[t] * (g[t] + 4.0 ** (-level) * beside[t]) for t in range(len(v))
        ]

    def residual_window(level, v, g):
        s, _, unit = window_refs[level]
        beside = beside_window(v, unit)
        return [
            g[t] - (4.0 ** (-level) * (4.0 * v[t] - beside[t]) + s[t] * v[t]) for t in range(len(v))
        ]

    for n, (dx, _, _) in enumerate(row_moves):
        @pl.when(inside(-dx, 0))
        def _():
            row_copy(n, -dx).wait_recv()

    own1, own_w = slice(base1, base1 + half_rows), slice(base_w, base_w + half_rows)
    g1[own_w, :] = gP[own1, :]
    s1[own_w, :] = sP[own1, :]
    w1[wide1, :] = weight(s1[wide1, :], ROWS_PAD - base_w, half_rows, cols // 2, half // 2, 1)
    a1[wide1, :] = w1[wide1, :] * g1[wide1, :]
    sweep_block(a1, b1, g1, w1, 1)
    put_strips(r1, wide1, s1[wide1, :])
    tiles = pack_window(r1)
    for t in range(4):
        s2w[t] = tiles[t]
        w2w[t] = jnp.where(in_domain(32), DAMPING / (4.0 ** (-1) + tiles[t]), 0.0)
    tiles = halved_window(tiles, 32)
    for t in range(2):
        s3w[t] = tiles[t]
        w3w[t] = jnp.where(in_domain(64), DAMPING / (4.0 ** (-2) + tiles[t]), 0.0)

    def coarse_copy(peer):
        return pltpu.make_async_remote_copy(
            src_ref=cbuf.at[me], dst_ref=cbuf.at[me], send_sem=coarse_sems.at[0], recv_sem=coarse_sems.at[1],
            device_id=(peer // gy_count, lax.rem(peer, gy_count)), device_id_type=MESH,
        )

    def coarse_wait(n):
        others = cbuf.at[pl.ds(0, total - 1)]
        pltpu.make_async_copy(others, others, coarse_sems.at[n]).wait()

    gather_wait(1)
    unpack(1, g2)
    e = fcycle(2)
    e = vcycle(2, e)
    add_level2(e, b1)
    sweep_block(b1, a1, g1, w1, 1)
    sweep_block(a1, b1, g1, w1, 1)
    sweep_block(b1, a1, g1, w1, 1)
    sweep_block(a1, b1, g1, w1, 1)
    residual_block(b1, r1, g1, s1, 1)
    source2 = pack_window(r1)
    v2 = sweep_window(2, [w2w[t] * source2[t] for t in range(4)], source2)
    source3 = halved_window(residual_window(2, v2, source2), 32)
    v3 = sweep_window(3, [w3w[t] * source3[t] for t in range(2)], source3)
    source4 = halved_window(residual_window(3, v3, source3), 64)[0]
    place = lax.rem(gy, 8) * 16
    mine = pltpu.roll(source4[4:12], lax.rem(place + lanes - 8, lanes), 1)
    lane_c = iota((8, lanes), 1)
    cbuf[me] = jnp.where((lane_c >= place) & (lane_c < place + 16), mine, 0.0)

    @pl.loop(0, total - 1)
    def _(k):
        odd = lax.rem(k, 2)
        coarse_copy(lax.rem(me + total + total // 2 + odd * ((k + 1) // 2) - (1 - odd) * (k // 2), total)).start()

    gather_sent(0)
    gather_sent(1)
    for n, (dx, dy, source, target) in enumerate(sends):
        @pl.when(inside(dx, dy))
        def _():
            halo_copy(n, dx, dy, source, target).wait_send()
    for n, (dx, _, _) in enumerate(row_moves):
        @pl.when(inside(dx, 0))
        def _():
            row_copy(n, dx).wait_send()
    coarse_wait(1)
    for x in range(gx_count):
        for u in range(gy_count // 8):
            first = x * gy_count + u * 8
            pairs = [cbuf[first + k] + cbuf[first + k + 1] for k in range(0, 8, 2)]
            g4[0, x * 8 : x * 8 + 8, u * lanes : (u + 1) * lanes] = (pairs[0] + pairs[1]) + (pairs[2] + pairs[3])
    e = coarse(None, True)
    e = e[0, pl.ds(pl.multiple_of(gx * 8, 8), 24), :][4 : 4 + window]
    e = pltpu.roll(e, lax.rem(q_count + 8 - gy * 16 + q_count, q_count), 1)[:, 0:lanes]
    e = jnp.where(in_domain(lanes), e, 0.0)
    e = e + pltpu.roll(e, 64, 1)
    v3 = [v3[t] + e for t in range(2)]
    v3 = sweep_window(3, sweep_window(3, v3, source3), source3)
    e = [v3[t] + pltpu.roll(v3[t], 32, 1) for t in range(2)]
    v2 = [v2[t] + e[t // 2] for t in range(4)]
    v2 = sweep_window(2, sweep_window(2, v2, source2), source2)
    raised = exact_dot(jnp.concatenate(v2, 0), up_w[...])
    for t in range(4):
        put_window(t, raised[t * window : (t + 1) * window])
    b1[wide1, :] = b1[wide1, :] + get_strips(r1, wide1)
    near_w = (base_w - 8, base_w + half_rows + 8)
    sweep_block(b1, a1, g1, w1, 1, near_w)
    sweep_block(a1, b1, g1, w1, 1, near_w)
    raised = exact_dot(b1[slice(*near_w), :], up0[...])
    put_strips(fine_add, pl.ds(0, ext1, 2), raised)
    put_strips(fine_add, pl.ds(1, ext1, 2), raised)
    for lo in range(ROWS_PAD, ext - ROWS_PAD, 8):
        at = slice(lo, lo + 8)
        vB[at, :] = vB[at, :] + get_strips(fine_add, at)
    sweep_block(vB, vA, gE, wE, 0)
    sweep_block(vA, vB, gE, wE, 0)
    for lo in range(0, rows, 8):
        mid, beside = around(vB, base + lo, 8)
        at = slice(base + lo, base + lo + 8)
        left = gE[at, :] - ((4.0 * mid - beside) + sE[at, :] * mid)
        out_ref[0, lo : lo + 8, :] = mid[:, 0:cols]
        out_ref[1, lo : lo + 8, :] = left[:, 0:cols]

    coarse_wait(0)


def solution(mesh):
    gx_count, gy_count = mesh.shape["gx"], mesh.shape["gy"]
    total = gx_count * gy_count

    def body(right_side, shift):
        rows, cols = right_side.shape
        assert cols == 256 and rows == 128 and gy_count % 8 == 0
        ext, width = rows + 2 * (HALO + ROWS_PAD), cols + 128
        ext1, width1 = ext // 2 + 2 * ROWS_PAD, 256
        wide1 = rows // 2 + 2 * (ROW_HALO + ROWS_PAD)
        window = rows // 16 + 8
        p, q = rows // 16 * gx_count, cols // 16 * gy_count
        V = pltpu.VMEM
        dma = pltpu.SemaphoreType.DMA
        big = [V((ext, width), F32)] * 5 + [V((width // 128, ext, 128), F32)]
        one = [V((ext1, width1), F32)] * 5
        one += [V((wide1, width1), F32)] * 5 + [V((width1 // 128, wide1, 128), F32)]
        levels = []
        for n in (16, 4, 1):
            levels += [V((n, p, q), F32)] * 3 + [V((n, p + 16, q), F32)] * 2
        scratch = (
            [V((rows, cols), F32)] * 2 + [dma((2,))]
            + big + one
            + [V((rows, 128), F32)] * 2 + [V((ext, 128), F32)] * 2
            + [V((width, width1), BF16), V((width1, width), BF16), V((width1, 128), BF16), V((4 * q, width1), BF16)]
            + [V((width1, 128), BF16), V((128, width1), BF16)]
            + [V((2, total, 16, 128), F32), V((total, 8, 128), F32)]
            + levels
            + [V((4, 24, width1), F32)]
            + [V((4, window, 128), F32)] * 2 + [V((2, window, 128), F32)] * 2
            + [dma((10,)), dma((10,)), dma((4,)), dma((4,)), dma((2, total)), dma((2, total)), dma((2,))]
        )
        out = jax.ShapeDtypeStruct((2,) + right_side.shape, F32)
        both = pl.pallas_call(
            functools.partial(kernel, gx_count, gy_count),
            out_shape=out,
            in_specs=[pl.BlockSpec(memory_space=pltpu.HBM)] * 2,
            out_specs=pl.BlockSpec(memory_space=pltpu.VMEM),
            scratch_shapes=scratch,
            compiler_params=pltpu.CompilerParams(
                collective_id=0, has_side_effects=True, vmem_limit_bytes=60*1024*1024
            ),
        )(right_side, shift)
        return both[0], both[1]

    spec = P("gx", "gy")
    return jax.shard_map(body, mesh=mesh, in_specs=(spec, spec), out_specs=(spec, spec), check_vma=False)
```

profile of v0, /device:TPU:0, one launch (start us, length us, event | category | flops | bytes accessed | tf_op | source)
XLA Modules:
  0.0 38.1 jit_solution(15417263306275694806)
XLA Ops:
  0.6 35.8 %shard_map.41 = f32[2,128,256]{2,1,0:T(8,128)} custom-call(f32[128,256]{1,0:T(8,128)} %g_hbm.1, f32[128,256]{1,0:T(8,128)} %s_hbm.1), custom_call_target="tpu_custom_call" | custom-call | tf_op jit(solution)/shard_map/pallas_call | solution.py:708
  36.4 1.7 %slice_bitcast_fusion = (f32[128,256]{1,0:T(8,128)}, f32[128,256]{1,0:T(8,128)}) fusion(f32[2,128,256]{2,1,0:T(8,128)} %shard_map.41), kind=kLoop, calls=%fused_computation | loop fusion | bytes 524288 | tf_op jit(solution)/shard_map/squeeze | solution.py:718
where the time goes:
time: 38.3 us; the launch traced here: 38.1 us
  Pallas kernels  35.8 us (93%)
  local copies, waits for them, and re-layouts  1.69 us (4%)
  between operations  0.64 us (2%)
    pallas_call x1, Pallas kernels, body(): pl.pallas_call(functools.partial(kernel, gx_count, gy_count), out_shape=o...  35.8 us
    squeeze x1, local copies, waits for them, and re-layouts, body(): return (both[0], both[1])  1.69 us

commit v1 on v0

--- a/solution.py
+++ b/solution.py
@@ -7,7 +7,6 @@
 from jax.experimental.pallas import tpu as pltpu
 from jax.sharding import PartitionSpec as P
 
-COARSE_SWEEPS = 6
 DAMPING = 0.8
 MESH = pl.DeviceIdType.MESH
 F32 = jnp.float32
@@ -48,8 +47,8 @@
     g1, s1, w1, a1, b1, r1,
     send_l, send_r, recv_l, recv_r,
     down0, up0, down1, spread, down_w, up_w,
-    rbuf, cbuf, s2, w2, g2, a2, b2, s3, w3, g3, a3, b3, s4, w4, g4, a4, b4, picked,
-    s2w, w2w, s3w, w3w,
+    rbuf, cbuf, s2, w2, g2, a2, b2, s3, w3, g3, a3, b3, s4, w4, g4, a4, picked,
+    s2w, w2w, s3w, w3w, hw4, phi, beside4,
     halo_send, halo_recv, row_send, row_recv, all_send, all_recv, coarse_sems,
 ):
     gx, gy = lax.axis_index("gx"), lax.axis_index("gy")
@@ -256,7 +255,7 @@
     for ref in (aP, bP, a1, b1):
         ref[0:ROWS_PAD, :] = jnp.zeros((ROWS_PAD, width1), F32)
         ref[ref.shape[0] - ROWS_PAD :, :] = jnp.zeros((ROWS_PAD, width1), F32)
-    for ref in (a2, b2, a3, b3, a4, b4):
+    for ref in (a2, b2, a3, b3, a4):
         for i in range(ref.shape[0]):
             ref[i, 0:8, :] = jnp.zeros((8, q_count), F32)
             ref[i, 8 + p_count : 16 + p_count, :] = jnp.zeros((8, q_count), F32)
@@ -392,7 +391,7 @@
             )
         return mid, (north + south) + (west + east)
 
-    level_refs = {2: (s2, w2, g2, a2, b2, 4), 3: (s3, w3, g3, a3, b3, 2), 4: (s4, w4, g4, a4, b4, 1)}
+    level_refs = {2: (s2, w2, g2, a2, b2, 4), 3: (s3, w3, g3, a3, b3, 2), 4: (s4, w4, g4, a4, None, 1)}
 
     def sweep(level, v, out):
         s, w, g, _, _, n = level_refs[level]
@@ -450,25 +449,59 @@
     row_q = iota((p_count, q_count), 0)
     edges = jnp.where(row_q == 0, 1.0, 0.0) + jnp.where(row_q == p_count - 1, 1.0, 0.0)
     edges = edges + jnp.where(lane_q == 0, 1.0, 0.0) + jnp.where(lane_q == q_count - 1, 1.0, 0.0)
-    per_unit = 1.0 / total_of(4.0 ** (-4) * edges + s4[0])
-
-    def coarse(v, from_zero):
-        if from_zero:
-            shifted = jnp.zeros((p_count, q_count), F32) + total_of(g4[0]) * per_unit
+    unit4 = 4.0 ** (-4) * edges + s4[0]
+    per_unit = 1.0 / total_of(unit4)
+
+    def shifted(x, reach):
+        out = {0: x}
+        for k in range(1, reach + 1):
+            out[k] = jnp.where(lane_q < q_count - k, pltpu.roll(x, q_count - k, 1), 0.0)
+            out[-k] = jnp.where(lane_q >= k, pltpu.roll(x, k, 1), 0.0)
+        return out
+
+    reach4 = 2
+    for k, values in shifted(4.0 ** (-4) * w4[0], reach4).items():
+        hw4[k + reach4] = values
+    for i in range(beside4.shape[0]):
+        beside4[i, 0:8, :] = jnp.zeros((8, q_count), F32)
+        beside4[i, 8 + p_count : 16 + p_count, :] = jnp.zeros((8, q_count), F32)
+
+    def fused_sweeps(v, source, count):
+        for turn in range(count):
+            reach = count - 1 - turn
+            new = {}
+            for k in range(-reach, reach + 1):
+                slot = (turn % 2) * 5 + k + reach4
+                beside4[slot, rows_q, :] = v[k]
+                along = beside4[slot, 7 : 7 + p_count, :] + beside4[slot, 9 : 9 + p_count, :]
+                value = (1.0 - DAMPING) * v[k] + hw4[k + reach4] * ((v[k - 1] + v[k + 1]) + along)
+                new[k] = value if source is None else value + source[k]
+            v = new
+        return v[0]
+
+    def six_sweeps(v, source):
+        return fused_sweeps(shifted(fused_sweeps(shifted(v, 3), source, 3), 3), source, 3)
+
+    phi[0] = six_sweeps(jnp.ones((p_count, q_count), F32), None)
+    phi[1] = six_sweeps(phi[0], None)
+    kept = 1.0 - per_unit * total_of(unit4 * phi[0])
+
+    def coarse(twice=False):
+        source = shifted(w4[0] * g4[0], 3)
+        v = fused_sweeps(source, source, 3)
+        v = fused_sweeps(shifted(v, 2), source, 2)
+        add = total_of(g4[0]) * per_unit
+        if twice:
+            again = add * kept - total_of(unit4 * v) * per_unit
+            v = six_sweeps(v, source) + add * phi[1] + again * phi[0]
         else:
-            mid, beside = sides(v, 1, 0, 0)
-            left = g4[0] - (4.0 ** (-4) * (4.0 * mid - beside) + s4[0] * mid)
-            shifted = mid + total_of(left) * per_unit
-        now, later = a4, b4
-        now[0, rows_q, :] = shifted
-        for _ in range(COARSE_SWEEPS):
-            sweep(4, now, later)
-            now, later = later, now
-        return now
+            v = v + add * phi[0]
+        a4[0, rows_q, :] = v
+        return a4
 
     def vcycle(level, v):
         if level == 4:
-            return coarse(v, v is None)
+            return coarse()
         _, _, _, a, b, n = level_refs[level]
         if v is None:
             first_sweep(level, a)
@@ -486,14 +519,14 @@
         return now
 
     def fcycle(level):
-        if level == 4:
-            return coarse(None, True)
         _, _, _, a, b, n = level_refs[level]
         first_sweep(level, a)
         sweep(level, a, b)
         restricted(level, b)
-        e = fcycle(level + 1)
-        e = vcycle(level + 1, e)
+        if level == 3:
+            e = coarse(True)
+        else:
+            e = vcycle(level + 1, fcycle(level + 1))
         correct(level, b, e)
         sweep(level, b, a)
         sweep(level, a, b)
@@ -637,7 +670,7 @@
             first = x * gy_count + u * 8
             pairs = [cbuf[first + k] + cbuf[first + k + 1] for k in range(0, 8, 2)]
             g4[0, x * 8 : x * 8 + 8, u * lanes : (u + 1) * lanes] = (pairs[0] + pairs[1]) + (pairs[2] + pairs[3])
-    e = coarse(None, True)
+    e = coarse()
     e = e[0, pl.ds(pl.multiple_of(gx * 8, 8), 24), :][4 : 4 + window]
     e = pltpu.roll(e, lax.rem(q_count + 8 - gy * 16 + q_count, q_count), 1)[:, 0:lanes]
     e = jnp.where(in_domain(lanes), e, 0.0)
@@ -691,7 +724,7 @@
         one += [V((wide1, width1), F32)] * 5 + [V((width1 // 128, wide1, 128), F32)]
         levels = []
         for n in (16, 4, 1):
-            levels += [V((n, p, q), F32)] * 3 + [V((n, p + 16, q), F32)] * 2
+            levels += [V((n, p, q), F32)] * 3 + [V((n, p + 16, q), F32)] * (2 if n > 1 else 1)
         scratch = (
             [V((rows, cols), F32)] * 2 + [dma((2,))]
             + big + one
@@ -702,9 +735,10 @@
             + levels
             + [V((4, 24, width1), F32)]
             + [V((4, window, 128), F32)] * 2 + [V((2, window, 128), F32)] * 2
+            + [V((5, p, q), F32), V((2, p, q), F32), V((10, p + 16, q), F32)]
             + [dma((10,)), dma((10,)), dma((4,)), dma((4,)), dma((2, total)), dma((2, total)), dma((2,))]
         )
-        out = jax.ShapeDtypeStruct((2,) + right_side.shape, F32)
+        out = pltpu.VMEM((2,) + right_side.shape, F32)
         both = pl.pallas_call(
             functools.partial(kernel, gx_count, gy_count),
             out_shape=out,

time: 38.3 us -> 34.9 us (0.911)
  Pallas kernels: 35.8 us -> 33.4 us
  local copies, waits for them, and re-layouts: 1.69 us -> 0.72 us
    pallas_call x1, Pallas kernels: 35.8 us -> 33.4 us  [body(): pl.pallas_call(functools.partial(kernel, gx_count, gy_count), out_shape=o...]
    squeeze x1, local copies, waits for them, and re-layouts: 1.69 us -> 0.72 us  [body(): return (both[0], both[1])]
where the time goes in v1:
time: 34.9 us; the launch traced here: 34.7 us
  Pallas kernels  33.4 us (96%)
  local copies, waits for them, and re-layouts  0.72 us (2%)
  between operations  0.64 us (2%)
    pallas_call x1, Pallas kernels, body(): pl.pallas_call(functools.partial(kernel, gx_count, gy_count), out_shape=o...  33.4 us
    squeeze x1, local copies, waits for them, and re-layouts, body(): return (both[0], both[1])  0.72 us

profile of v1, /device:TPU:0, one launch (start us, length us, event | category | flops | bytes accessed | tf_op | source)
XLA Modules:
  0.0 34.7 jit_solution(14094902129014930446)
XLA Ops:
  0.6 33.4 %shard_map.41 = f32[2,128,256]{2,1,0:T(8,128)S(1)} custom-call(f32[128,256]{1,0:T(8,128)} %g_hbm.1, f32[128,256]{1,0:T(8,128)} %s_hbm.1), custom_call_target="tpu_custom_call" | custom-call | tf_op jit(solution)/shard_map/pallas_call | solution.py:742
  34.0 0.7 %slice_bitcast_fusion = (f32[128,256]{1,0:T(8,128)}, f32[128,256]{1,0:T(8,128)}) fusion(f32[2,128,256]{2,1,0:T(8,128)S(1)} %shard_map.41), kind=kLoop, calls=%fused_computation | loop fusion | bytes 524288 | tf_op jit(solution)/shard_map/squeeze | solution.py:752

commit v2 on v1

--- a/solution.py
+++ b/solution.py
@@ -49,7 +49,7 @@
     down0, up0, down1, spread, down_w, up_w,
     rbuf, cbuf, s2, w2, g2, a2, b2, s3, w3, g3, a3, b3, s4, w4, g4, a4, picked,
     s2w, w2w, s3w, w3w, hw4, phi, beside4,
-    halo_send, halo_recv, row_send, row_recv, all_send, all_recv, coarse_sems,
+    halo_send, halo_recv, row_send, row_recv, all_send, all_recv, coarse_sems, row_wave,
 ):
     gx, gy = lax.axis_index("gx"), lax.axis_index("gy")
     total = gx_count * gy_count
@@ -78,14 +78,36 @@
     for ref in (g1, s1):
         ref[0:base_w, :] = jnp.zeros((base_w, width1), F32)
         ref[base_w + half_rows :, :] = jnp.zeros((base_w, width1), F32)
+    def inside(dx, dy):
+        ok = None
+        for step, at, count in ((dx, gx, gx_count), (dy, gy, gy_count)):
+            if step:
+                here = (at > 0) if step < 0 else (at < count - 1)
+                ok = here if ok is None else ok & here
+        return ok
+
+    def wrap(at, step, count):
+        return lax.rem(at + count + step, count)
+
+    def each(count, body):
+        if count <= 64:
+            for j in range(1, count):
+                body(j)
+        else:
+            pl.loop(1, count)(body)
+
     barrier = pltpu.get_barrier_semaphore()
-
-    @pl.loop(1, total)
-    def _(k):
-        peer = lax.rem(me + k, total)
-        pl.semaphore_signal(
-            barrier, inc=1, device_id=(peer // gy_count, lax.rem(peer, gy_count)), device_id_type=MESH
-        )
+    beyond = [(dx, dy) for dx in (-1, 1) for dy in (0, -1, 1)]
+
+    def greet(x, y):
+        pl.semaphore_signal(barrier, inc=1, device_id=(x, y), device_id_type=MESH)
+
+    for dx, dy in beyond:
+        @pl.when(inside(dx, dy))
+        def _():
+            greet(gx + dx, gy + dy)
+
+    each(gy_count, lambda k: greet(gx, wrap(gy, k, gy_count)))
 
     lane = iota((rows, lanes), 1)
     half = lanes // 2
@@ -156,7 +178,12 @@
     gE[base : base + rows, 0:cols] = g_ref[...]
     sE[base : base + rows, 0:cols] = s_ref[...]
 
-    pl.semaphore_wait(barrier, total - 1)
+    def beside_count(at, count):
+        return (at + count - 1) // count + 1 - (at + 1) // count
+
+    pl.semaphore_wait(
+        barrier, gy_count - 1 + beside_count(gx, gx_count) * (1 + beside_count(gy, gy_count))
+    )
 
     top, bottom = slice(0, HALO), slice(rows - HALO, rows)
     above, below = slice(ROWS_PAD, base), slice(base + rows, base + rows + HALO)
@@ -174,14 +201,6 @@
         (1, 0, s_ref.at[bottom, :], sE.at[above, 0:cols]),
     )
 
-    def inside(dx, dy):
-        ok = None
-        for step, at, count in ((dx, gx, gx_count), (dy, gy, gy_count)):
-            if step:
-                here = (at > 0) if step < 0 else (at < count - 1)
-                ok = here if ok is None else ok & here
-        return ok
-
     def halo_copy(n, dx, dy, source, target):
         return pltpu.make_async_remote_copy(
             src_ref=source, dst_ref=target, send_sem=halo_send.at[n], recv_sem=halo_recv.at[n],
@@ -193,15 +212,33 @@
         def _():
             halo_copy(n, dx, dy, source, target).start()
 
+    def pass_on(n, step):
+        @pl.when(inside(-step, 0))
+        def _():
+            pl.semaphore_wait(row_wave.at[n], 1)
+
+        @pl.when(inside(step, 0))
+        def _():
+            pl.semaphore_signal(row_wave.at[n], inc=1, device_id=(gx + step, gy), device_id_type=MESH)
+
+    @pl.when(gx < gx_count // 2)
+    def _():
+        pass_on(0, 1)
+        pass_on(1, -1)
+
+    @pl.when(gx >= gx_count // 2)
+    def _():
+        pass_on(1, -1)
+        pass_on(0, 1)
+
     core = lax.rem(gy, 2)
     per_row = gy_count // 2
     chips = total // 2
-    chip = me // 2
     partner = (gx, gy + 1 - 2 * core)
 
-    def zigzag(j):
-        odd = lax.rem(j, 2)
-        return odd * ((j + 1) // 2) + (1 - odd) * (chips - j // 2)
+    def zigzag(j, count):
+        odd = j % 2
+        return odd * ((j + 1) // 2) + (1 - odd) * (count - j // 2)
 
     def block_copy(turn, n, slot, peer):
         return pltpu.make_async_remote_copy(
@@ -211,41 +248,38 @@
         )
 
     def direct(turn, j):
-        other = lax.rem(chip + zigzag(j), chips)
-        return block_copy(turn, j, me, (other // per_row, 2 * lax.rem(other, per_row) + core))
+        n = zigzag(j, chips)
+        peer = (wrap(gx, n // per_row, gx_count), wrap(gy, 2 * (n % per_row), gy_count))
+        return block_copy(turn, j, me, peer)
+
+    def sender(j):
+        n = zigzag(j, chips)
+        return wrap(gx, -(n // per_row), gx_count) * gy_count + wrap(gy, -2 * (n % per_row), gy_count)
 
     def onward(turn, j):
-        slot = 2 * lax.rem(chip + chips - zigzag(j), chips) + core
-        return block_copy(turn, chips + j, slot, partner)
+        return block_copy(turn, chips + j, sender(j), partner)
 
     def gather_start(turn):
         block_copy(turn, 0, me, partner).start()
-
-        @pl.loop(1, chips)
-        def _(j):
-            direct(turn, chips - j).start()
+        each(chips, lambda j: direct(turn, chips - j).start())
 
     def gather_wait(turn):
-        @pl.loop(1, chips)
-        def _(j):
+        def pass_block(j):
             copy = onward(turn, j)
             copy.wait_recv()
             copy.start()
 
+        each(chips, pass_block)
         block_copy(turn, 0, me + 1 - 2 * core, partner).wait_recv()
-
-        @pl.loop(1, chips)
-        def _(j):
-            slot = 2 * lax.rem(chip + chips - zigzag(j), chips) + 1 - core
-            block_copy(turn, chips + j, slot, partner).wait_recv()
+        each(chips, lambda j: block_copy(turn, chips + j, sender(j) + 1 - 2 * core, partner).wait_recv())
 
     def gather_sent(turn):
-        block_copy(turn, 0, me, partner).wait_send()
-
-        @pl.loop(1, chips)
-        def _(j):
+        def sent(j):
             direct(turn, j).wait_send()
             onward(turn, j).wait_send()
+
+        block_copy(turn, 0, me, partner).wait_send()
+        each(chips, sent)
 
     gather_start(0)
     zero_tile = jnp.zeros((ROWS_PAD, width), F32)
@@ -619,11 +653,12 @@
         s3w[t] = tiles[t]
         w3w[t] = jnp.where(in_domain(64), DAMPING / (4.0 ** (-2) + tiles[t]), 0.0)
 
-    def coarse_copy(peer):
-        return pltpu.make_async_remote_copy(
+    def coarse_send(k):
+        n = zigzag(total - k, total)
+        pltpu.make_async_remote_copy(
             src_ref=cbuf.at[me], dst_ref=cbuf.at[me], send_sem=coarse_sems.at[0], recv_sem=coarse_sems.at[1],
-            device_id=(peer // gy_count, lax.rem(peer, gy_count)), device_id_type=MESH,
-        )
+            device_id=(wrap(gx, n // gy_count, gx_count), wrap(gy, n % gy_count, gy_count)), device_id_type=MESH,
+        ).start()
 
     def coarse_wait(n):
         others = cbuf.at[pl.ds(0, total - 1)]
@@ -649,11 +684,7 @@
     lane_c = iota((8, lanes), 1)
     cbuf[me] = jnp.where((lane_c >= place) & (lane_c < place + 16), mine, 0.0)
 
-    @pl.loop(0, total - 1)
-    def _(k):
-        odd = lax.rem(k, 2)
-        coarse_copy(lax.rem(me + total + total // 2 + odd * ((k + 1) // 2) - (1 - odd) * (k // 2), total)).start()
-
+    each(total, coarse_send)
     gather_sent(0)
     gather_sent(1)
     for n, (dx, dy, source, target) in enumerate(sends):
@@ -737,6 +768,7 @@
             + [V((4, window, 128), F32)] * 2 + [V((2, window, 128), F32)] * 2
             + [V((5, p, q), F32), V((2, p, q), F32), V((10, p + 16, q), F32)]
             + [dma((10,)), dma((10,)), dma((4,)), dma((4,)), dma((2, total)), dma((2, total)), dma((2,))]
+            + [pltpu.SemaphoreType.REGULAR((2,))]
         )
         out = pltpu.VMEM((2,) + right_side.shape, F32)
         both = pl.pallas_call(

time: 34.9 us -> 33.4 us (0.957)
  Pallas kernels: 33.4 us -> 31.9 us
    pallas_call x1, Pallas kernels: 33.4 us -> 31.9 us  [body(): pl.pallas_call(functools.partial(kernel, gx_count, gy_count), out_shape=o...]
where the time goes in v2:
time: 33.4 us; the launch traced here: 33.3 us
  Pallas kernels  31.9 us (96%)
  local copies, waits for them, and re-layouts  0.72 us (2%)
  between operations  0.64 us (2%)
    pallas_call x1, Pallas kernels, body(): pl.pallas_call(functools.partial(kernel, gx_count, gy_count), out_shape=o...  31.9 us
    squeeze x1, local copies, waits for them, and re-layouts, body(): return (both[0], both[1])  0.72 us

profile of v2, /device:TPU:0, one launch (start us, length us, event | category | flops | bytes accessed | tf_op | source)
XLA Modules:
  0.0 33.3 jit_solution(11644844634162027350)
XLA Ops:
  0.6 31.9 %shard_map.41 = f32[2,128,256]{2,1,0:T(8,128)S(1)} custom-call(f32[128,256]{1,0:T(8,128)} %g_hbm.1, f32[128,256]{1,0:T(8,128)} %s_hbm.1), custom_call_target="tpu_custom_call" | custom-call | tf_op jit(solution)/shard_map/pallas_call | solution.py:774
  32.6 0.7 %slice_bitcast_fusion = (f32[128,256]{1,0:T(8,128)}, f32[128,256]{1,0:T(8,128)}) fusion(f32[2,128,256]{2,1,0:T(8,128)S(1)} %shard_map.41), kind=kLoop, calls=%fused_computation | loop fusion | bytes 524288 | tf_op jit(solution)/shard_map/squeeze | solution.py:784

commit v3 on v2

--- a/solution.py
+++ b/solution.py
@@ -97,12 +97,13 @@
             pl.loop(1, count)(body)
 
     barrier = pltpu.get_barrier_semaphore()
-    beyond = [(dx, dy) for dx in (-1, 1) for dy in (0, -1, 1)]
+    corners = [(dx, dy) for dx in (-1, 1) for dy in (-1, 1)]
 
     def greet(x, y):
         pl.semaphore_signal(barrier, inc=1, device_id=(x, y), device_id_type=MESH)
 
-    for dx, dy in beyond:
+    each(gx_count, lambda k: greet(wrap(gx, k, gx_count), gy))
+    for dx, dy in corners:
         @pl.when(inside(dx, dy))
         def _():
             greet(gx + dx, gy + dy)
@@ -168,29 +169,22 @@
         low = iota((16, lanes), 1) < half
         return jnp.where(low, means[0:16], means[16:32])
 
-    own_strips = cols // lanes
-    for k in range(own_strips):
-        fine_add[k, base : base + rows, :] = s_ref[:, k * lanes : (k + 1) * lanes]
-    own = get_strips(fine_add, pl.ds(base, half_rows, 2), own_strips)
-    own = own + get_strips(fine_add, pl.ds(base + 1, half_rows, 2), own_strips)
-    put_strips(r1, slice(base1, base1 + half_rows), 0.25 * exact_dot(own, down0[0:cols, :]))
-    rbuf[0, me] = pack_level2(r1)
-    gE[base : base + rows, 0:cols] = g_ref[...]
-    sE[base : base + rows, 0:cols] = s_ref[...]
-
     def beside_count(at, count):
         return (at + count - 1) // count + 1 - (at + 1) // count
 
     pl.semaphore_wait(
-        barrier, gy_count - 1 + beside_count(gx, gx_count) * (1 + beside_count(gy, gy_count))
+        barrier, gx_count + gy_count - 2 + beside_count(gx, gx_count) * beside_count(gy, gy_count)
     )
+
+    def tell_row(k):
+        pl.semaphore_signal(row_wave, inc=1, device_id=(wrap(gx, k, gx_count), gy), device_id_type=MESH)
+
+    each(gx_count, tell_row)
 
     top, bottom = slice(0, HALO), slice(rows - HALO, rows)
     above, below = slice(ROWS_PAD, base), slice(base + rows, base + rows + HALO)
     middle = slice(base, base + rows)
     sends = (
-        (0, -1, send_l, recv_r.at[middle, :]),
-        (0, 1, send_r, recv_l.at[middle, :]),
         (-1, -1, send_l.at[top, :], recv_r.at[below, :]),
         (1, -1, send_l.at[bottom, :], recv_r.at[above, :]),
         (-1, 1, send_r.at[top, :], recv_l.at[below, :]),
@@ -199,6 +193,8 @@
         (-1, 0, s_ref.at[top, :], sE.at[below, 0:cols]),
         (1, 0, g_ref.at[bottom, :], gE.at[above, 0:cols]),
         (1, 0, s_ref.at[bottom, :], sE.at[above, 0:cols]),
+        (0, -1, send_l, recv_r.at[middle, :]),
+        (0, 1, send_r, recv_l.at[middle, :]),
     )
 
     def halo_copy(n, dx, dy, source, target):
@@ -211,25 +207,6 @@
         @pl.when(inside(dx, dy))
         def _():
             halo_copy(n, dx, dy, source, target).start()
-
-    def pass_on(n, step):
-        @pl.when(inside(-step, 0))
-        def _():
-            pl.semaphore_wait(row_wave.at[n], 1)
-
-        @pl.when(inside(step, 0))
-        def _():
-            pl.semaphore_signal(row_wave.at[n], inc=1, device_id=(gx + step, gy), device_id_type=MESH)
-
-    @pl.when(gx < gx_count // 2)
-    def _():
-        pass_on(0, 1)
-        pass_on(1, -1)
-
-    @pl.when(gx >= gx_count // 2)
-    def _():
-        pass_on(1, -1)
-        pass_on(0, 1)
 
     core = lax.rem(gy, 2)
     per_row = gy_count // 2
@@ -281,7 +258,70 @@
         block_copy(turn, 0, me, partner).wait_send()
         each(chips, sent)
 
-    gather_start(0)
+    def slot_of(d, j):
+        return wrap(gx, -d, gx_count) * gy_count + wrap(gy, -2 * j, gy_count)
+
+    def each_block(first_d, first_j, body):
+        if total <= 64:
+            for d in range(first_d, gx_count):
+                for j in range(first_j, per_row):
+                    body(d, j)
+        else:
+            pl.loop(first_d, gx_count)(lambda d: pl.loop(first_j, per_row)(lambda j: body(d, j)))
+
+    def along_line(turn, d):
+        return block_copy(turn, d, me, (wrap(gx, d, gx_count), gy))
+
+    def across(turn, d, j):
+        n = gx_count + d * (per_row - 1) + j - 1
+        return block_copy(turn, n, slot_of(d, 0), (gx, wrap(gy, 2 * j, gy_count)))
+
+    def to_partner(turn, d, j):
+        return block_copy(turn, chips + d * per_row + j, slot_of(d, j), partner)
+
+    def from_partner(turn, d, j):
+        return block_copy(turn, 0, slot_of(d, j) + 1 - 2 * core, partner)
+
+    def line_start(turn):
+        block_copy(turn, 0, me, partner).start()
+        each(gx_count, lambda d: along_line(turn, gx_count - d).start())
+        each(per_row, lambda j: across(turn, 0, per_row - j).start())
+
+    def line_pass(turn):
+        def pass_line(d):
+            block_copy(turn, 0, slot_of(d, 0), partner).wait_recv()
+            each(per_row, lambda j: across(turn, d, per_row - j).start())
+            to_partner(turn, d, 0).start()
+
+        each(gx_count, pass_line)
+
+    def line_wait(turn):
+        def pass_block(d, j):
+            copy = to_partner(turn, d, j)
+            copy.wait_recv()
+            copy.start()
+
+        each_block(0, 1, pass_block)
+        each_block(0, 0, lambda d, j: from_partner(turn, d, j).wait_recv())
+
+    def line_sent(turn):
+        block_copy(turn, 0, me, partner).wait_send()
+        each(gx_count, lambda d: along_line(turn, d).wait_send())
+        each_block(0, 1, lambda d, j: across(turn, d, j).wait_send())
+        each_block(1, 0, lambda d, j: to_partner(turn, d, j).wait_send())
+        each(per_row, lambda j: to_partner(turn, 0, j).wait_send())
+
+    gE[base : base + rows, 0:cols] = g_ref[...]
+    sE[base : base + rows, 0:cols] = s_ref[...]
+
+    own_strips = cols // lanes
+    for k in range(own_strips):
+        fine_add[k, base : base + rows, :] = s_ref[:, k * lanes : (k + 1) * lanes]
+    own = get_strips(fine_add, pl.ds(base, half_rows, 2), own_strips)
+    own = own + get_strips(fine_add, pl.ds(base + 1, half_rows, 2), own_strips)
+    put_strips(r1, slice(base1, base1 + half_rows), 0.25 * exact_dot(own, down0[0:cols, :]))
+    rbuf[0, me] = pack_level2(r1)
+    line_start(0)
     zero_tile = jnp.zeros((ROWS_PAD, width), F32)
     for ref in (vA, vB):
         ref[0:ROWS_PAD, :] = zero_tile
@@ -377,8 +417,9 @@
     sweep_block(aP, bP, gP, wP, 1)
     residual_block(bP, r1, gP, sP, 1, (base1, base1 + half_rows))
     rbuf[1, me] = pack_level2(r1)
+    pl.semaphore_wait(row_wave, gx_count - 1)
     gather_start(1)
-    rows_start((2, 3))
+    line_pass(0)
 
     block = (lane_e[0:8] // 16)
 
@@ -476,7 +517,94 @@
     def total_of(x):
         return jnp.sum(jnp.sum(x, axis=0, keepdims=True), axis=1, keepdims=True)
 
-    gather_wait(0)
+    window = picked.shape[1] - 8
+    lane_w, row_w = iota((window, lanes), 1), iota((window, lanes), 0)
+
+    def in_domain(period):
+        at_p, at_q = gx * 8 - 4 + row_w, gy * 16 - 8 + lane_w % period
+        good = (at_p >= 0) & (at_p < p_count) & (at_q >= 0) & (at_q < q_count)
+        return good & (lane_w % period < 32)
+
+    def put_window(t, values):
+        for a in range(2):
+            put_strips(r1, pl.ds(ROWS_PAD + 2 * t + a, window, 8), values)
+
+    def add_level2(e, v):
+        for t in range(4):
+            tiles = [e[t * 4 + r, pl.ds(pl.multiple_of(gx * 8, 8), 24), :] for r in range(4)]
+            picked[t] = exact_dot(jnp.concatenate(tiles, 1), spread[...])
+        for t in range(4):
+            put_window(t, picked[t, 4 : 4 + window, :])
+        v[wide1, :] = v[wide1, :] + get_strips(r1, wide1)
+
+    def pack_window(source):
+        parts = []
+        for t in range(4):
+            start = ROWS_PAD + 2 * t
+            parts.append(
+                get_strips(source, pl.ds(start, window, 8)) + get_strips(source, pl.ds(start + 1, window, 8))
+            )
+        means = 0.25 * exact_dot(jnp.concatenate(parts, 0), down_w[...])
+        return [means[t * window : (t + 1) * window] for t in range(4)]
+
+    def joined(x, unit):
+        return x + pltpu.roll(x, lanes - unit, 1)
+
+    def halved_window(tiles, unit):
+        return [0.25 * joined(tiles[2 * t] + tiles[2 * t + 1], unit) for t in range(len(tiles) // 2)]
+
+    def beside_window(v, unit):
+        n = len(v)
+        out = []
+        for t in range(n):
+            north = v[t - 1] if t > 0 else pltpu.roll(v[n - 1], 1, 0)
+            south = v[t + 1] if t < n - 1 else pltpu.roll(v[0], window - 1, 0)
+            west = jnp.where(lane_w < unit, pltpu.roll(v[t], unit + 1, 1), pltpu.roll(v[t], unit, 1))
+            east = jnp.where(
+                lane_w >= lanes - unit,
+                pltpu.roll(v[t], lanes - unit - 1, 1), pltpu.roll(v[t], lanes - unit, 1),
+            )
+            out.append((north + south) + (west + east))
+        return out
+
+    window_refs = {2: (s2w, w2w, 32), 3: (s3w, w3w, 64)}
+
+    def sweep_window(level, v, g):
+        _, w, unit = window_refs[level]
+        beside = beside_window(v, unit)
+        return [
+            (1.0 - DAMPING) * v[t] + w[t] * (g[t] + 4.0 ** (-level) * beside[t]) for t in range(len(v))
+        ]
+
+    def residual_window(level, v, g):
+        s, _, unit = window_refs[level]
+        beside = beside_window(v, unit)
+        return [
+            g[t] - (4.0 ** (-level) * (4.0 * v[t] - beside[t]) + s[t] * v[t]) for t in range(len(v))
+        ]
+
+    def rows_wait(which):
+        for n in which:
+            dx = row_moves[n][0]
+            @pl.when(inside(-dx, 0))
+            def _():
+                row_copy(n, -dx).wait_recv()
+
+    own1, own_w = slice(base1, base1 + half_rows), slice(base_w, base_w + half_rows)
+    rows_wait((0, 1))
+    s1[own_w, :] = sP[own1, :]
+    w1[wide1, :] = weight(s1[wide1, :], ROWS_PAD - base_w, half_rows, cols // 2, half // 2, 1)
+    put_strips(r1, wide1, s1[wide1, :])
+    tiles = pack_window(r1)
+    for t in range(4):
+        s2w[t] = tiles[t]
+        w2w[t] = jnp.where(in_domain(32), DAMPING / (4.0 ** (-1) + tiles[t]), 0.0)
+    tiles = halved_window(tiles, 32)
+    for t in range(2):
+        s3w[t] = tiles[t]
+        w3w[t] = jnp.where(in_domain(64), DAMPING / (4.0 ** (-2) + tiles[t]), 0.0)
+
+    line_wait(0)
     unpack(0, s2)
     for level in (2, 3, 4):
         prepare(level)
@@ -500,12 +628,12 @@
         beside4[i, 0:8, :] = jnp.zeros((8, q_count), F32)
         beside4[i, 8 + p_count : 16 + p_count, :] = jnp.zeros((8, q_count), F32)
 
-    def fused_sweeps(v, source, count):
+    def fused_sweeps(v, source, count, first_slot=0):
         for turn in range(count):
             reach = count - 1 - turn
             new = {}
             for k in range(-reach, reach + 1):
-                slot = (turn % 2) * 5 + k + reach4
+                slot = first_slot + (turn % 2) * 5 + k + reach4
                 beside4[slot, rows_q, :] = v[k]
                 along = beside4[slot, 7 : 7 + p_count, :] + beside4[slot, 9 : 9 + p_count, :]
                 value = (1.0 - DAMPING) * v[k] + hw4[k + reach4] * ((v[k - 1] + v[k + 1]) + along)
@@ -513,12 +641,9 @@
             v = new
         return v[0]
 
-    def six_sweeps(v, source):
-        return fused_sweeps(shifted(fused_sweeps(shifted(v, 3), source, 3), 3), source, 3)
-
-    phi[0] = six_sweeps(jnp.ones((p_count, q_count), F32), None)
-    phi[1] = six_sweeps(phi[0], None)
-    kept = 1.0 - per_unit * total_of(unit4 * phi[0])
+    def six_sweeps(v, source, first_slot=0):
+        v = fused_sweeps(shifted(v, 3), source, 3, first_slot)
+        return fused_sweeps(shifted(v, 3), source, 3, first_slot)
 
     def coarse(twice=False):
         source = shifted(w4[0] * g4[0], 3)
@@ -526,6 +651,9 @@
         v = fused_sweeps(shifted(v, 2), source, 2)
         add = total_of(g4[0]) * per_unit
         if twice:
+            phi[0] = six_sweeps(jnp.ones((p_count, q_count), F32), None, 10)
+            phi[1] = six_sweeps(phi[0], None, 10)
+            kept = 1.0 - per_unit * total_of(unit4 * phi[0])
             again = add * kept - total_of(unit4 * v) * per_unit
             v = six_sweeps(v, source) + add * phi[1] + again * phi[0]
         else:
@@ -566,93 +694,6 @@
         sweep(level, a, b)
         return b
 
-    window = picked.shape[1] - 8
-    lane_w, row_w = iota((window, lanes), 1), iota((window, lanes), 0)
-
-    def in_domain(period):
-        at_p, at_q = gx * 8 - 4 + row_w, gy * 16 - 8 + lane_w % period
-        good = (at_p >= 0) & (at_p < p_count) & (at_q >= 0) & (at_q < q_count)
-        return good & (lane_w % period < 32)
-
-    def put_window(t, values):
-        for a in range(2):
-            put_strips(r1, pl.ds(ROWS_PAD + 2 * t + a, window, 8), values)
-
-    def add_level2(e, v):
-        for t in range(4):
-            tiles = [e[t * 4 + r, pl.ds(pl.multiple_of(gx * 8, 8), 24), :] for r in range(4)]
-            picked[t] = exact_dot(jnp.concatenate(tiles, 1), spread[...])
-        for t in range(4):
-            put_window(t, picked[t, 4 : 4 + window, :])
-        v[wide1, :] = v[wide1, :] + get_strips(r1, wide1)
-
-    def pack_window(source):
-        parts = []
-        for t in range(4):
-            start = ROWS_PAD + 2 * t
-            parts.append(
-                get_strips(source, pl.ds(start, window, 8)) + get_strips(source, pl.ds(start + 1, window, 8))
-            )
-        means = 0.25 * exact_dot(jnp.concatenate(parts, 0), down_w[...])
-        return [means[t * window : (t + 1) * window] for t in range(4)]
-
-    def joined(x, unit):
-        return x + pltpu.roll(x, lanes - unit, 1)
-
-    def halved_window(tiles, unit):
-        return [0.25 * joined(tiles[2 * t] + tiles[2 * t + 1], unit) for t in range(len(tiles) // 2)]
-
-    def beside_window(v, unit):
-        n = len(v)
-        out = []
-        for t in range(n):
-            north = v[t - 1] if t > 0 else pltpu.roll(v[n - 1], 1, 0)
-            south = v[t + 1] if t < n - 1 else pltpu.roll(v[0], window - 1, 0)
-            west = jnp.where(lane_w < unit, pltpu.roll(v[t], unit + 1, 1), pltpu.roll(v[t], unit, 1))
-            east = jnp.where(
-                lane_w >= lanes - unit,
-                pltpu.roll(v[t], lanes - unit - 1, 1), pltpu.roll(v[t], lanes - unit, 1),
-            )
-            out.append((north + south) + (west + east))
-        return out
-
-    window_refs = {2: (s2w, w2w, 32), 3: (s3w, w3w, 64)}
-
-    def sweep_window(level, v, g):
-        _, w, unit = window_refs[level]
-        beside = beside_window(v, unit)
-        return [
-            (1.0 - DAMPING) * v[t] + w[t] * (g[t] + 4.0 ** (-level) * beside[t]) for t in range(len(v))
-        ]
-
-    def residual_window(level, v, g):
-        s, _, unit = window_refs[level]
-        beside = beside_window(v, unit)
-        return [
-            g[t] - (4.0 ** (-level) * (4.0 * v[t] - beside[t]) + s[t] * v[t]) for t in range(len(v))
-        ]
-
-    for n, (dx, _, _) in enumerate(row_moves):
-        @pl.when(inside(-dx, 0))
-        def _():
-            row_copy(n, -dx).wait_recv()
-
-    own1, own_w = slice(base1, base1 + half_rows), slice(base_w, base_w + half_rows)
-    g1[own_w, :] = gP[own1, :]
-    s1[own_w, :] = sP[own1, :]
-    w1[wide1, :] = weight(s1[wide1, :], ROWS_PAD - base_w, half_rows, cols // 2, half // 2, 1)
-    a1[wide1, :] = w1[wide1, :] * g1[wide1, :]
-    sweep_block(a1, b1, g1, w1, 1)
-    put_strips(r1, wide1, s1[wide1, :])
-    tiles = pack_window(r1)
-    for t in range(4):
-        s2w[t] = tiles[t]
-        w2w[t] = jnp.where(in_domain(32), DAMPING / (4.0 ** (-1) + tiles[t]), 0.0)
-    tiles = halved_window(tiles, 32)
-    for t in range(2):
-        s3w[t] = tiles[t]
-        w3w[t] = jnp.where(in_domain(64), DAMPING / (4.0 ** (-2) + tiles[t]), 0.0)
-
     def coarse_send(k):
         n = zigzag(total - k, total)
         pltpu.make_async_remote_copy(
@@ -665,9 +706,14 @@
         pltpu.make_async_copy(others, others, coarse_sems.at[n]).wait()
 
     gather_wait(1)
+    rows_start((2, 3))
     unpack(1, g2)
     e = fcycle(2)
     e = vcycle(2, e)
+    rows_wait((2, 3))
+    g1[own_w, :] = gP[own1, :]
+    a1[wide1, :] = w1[wide1, :] * g1[wide1, :]
+    sweep_block(a1, b1, g1, w1, 1)
     add_level2(e, b1)
     sweep_block(b1, a1, g1, w1, 1)
     sweep_block(a1, b1, g1, w1, 1)
@@ -685,7 +731,7 @@
     cbuf[me] = jnp.where((lane_c >= place) & (lane_c < place + 16), mine, 0.0)
 
     each(total, coarse_send)
-    gather_sent(0)
+    line_sent(0)
     gather_sent(1)
     for n, (dx, dy, source, target) in enumerate(sends):
         @pl.when(inside(dx, dy))
@@ -766,9 +812,9 @@
             + levels
             + [V((4, 24, width1), F32)]
             + [V((4, window, 128), F32)] * 2 + [V((2, window, 128), F32)] * 2
-            + [V((5, p, q), F32), V((2, p, q), F32), V((10, p + 16, q), F32)]
+            + [V((5, p, q), F32), V((2, p, q), F32), V((20, p + 16, q), F32)]
             + [dma((10,)), dma((10,)), dma((4,)), dma((4,)), dma((2, total)), dma((2, total)), dma((2,))]
-            + [pltpu.SemaphoreType.REGULAR((2,))]
+            + [pltpu.SemaphoreType.REGULAR]
         )
         out = pltpu.VMEM((2,) + right_side.shape, F32)
         both = pl.pallas_call(

time: 33.4 us -> 32 us (0.958)
  Pallas kernels: 31.9 us -> 30.5 us
    pallas_call x1, Pallas kernels: 31.9 us -> 30.5 us  [body(): pl.pallas_call(functools.partial(kernel, gx_count, gy_count), out_shape=o...]
where the time goes in v3:
time: 32 us; the launch traced here: 31.9 us
  Pallas kernels  30.5 us (95%)
  local copies, waits for them, and re-layouts  0.72 us (2%)
  between operations  0.64 us (2%)
    pallas_call x1, Pallas kernels, body(): pl.pallas_call(functools.partial(kernel, gx_count, gy_count), out_shape=o...  30.5 us
    squeeze x1, local copies, waits for them, and re-layouts, body(): return (both[0], both[1])  0.72 us

profile of v3, /device:TPU:0, one launch (start us, length us, event | category | flops | bytes accessed | tf_op | source)
XLA Modules:
  0.0 31.9 jit_solution(10074968662195491337)
XLA Ops:
  0.6 30.5 %shard_map.41 = f32[2,128,256]{2,1,0:T(8,128)S(1)} custom-call(f32[128,256]{1,0:T(8,128)} %g_hbm.1, f32[128,256]{1,0:T(8,128)} %s_hbm.1), custom_call_target="tpu_custom_call" | custom-call | tf_op jit(solution)/shard_map/pallas_call | solution.py:820
  31.2 0.7 %slice_bitcast_fusion = (f32[128,256]{1,0:T(8,128)}, f32[128,256]{1,0:T(8,128)}) fusion(f32[2,128,256]{2,1,0:T(8,128)S(1)} %shard_map.41), kind=kLoop, calls=%fused_computation | loop fusion | bytes 524288 | tf_op jit(solution)/shard_map/squeeze | solution.py:830

commit v4 on v3

--- a/solution.py
+++ b/solution.py
@@ -49,7 +49,7 @@
     down0, up0, down1, spread, down_w, up_w,
     rbuf, cbuf, s2, w2, g2, a2, b2, s3, w3, g3, a3, b3, s4, w4, g4, a4, picked,
     s2w, w2w, s3w, w3w, hw4, phi, beside4,
-    halo_send, halo_recv, row_send, row_recv, all_send, all_recv, coarse_sems, row_wave,
+    halo_send, halo_recv, row_send, row_recv, all_send, all_recv, coarse_sems, told,
 ):
     gx, gy = lax.axis_index("gx"), lax.axis_index("gy")
     total = gx_count * gy_count
@@ -108,7 +108,18 @@
         def _():
             greet(gx + dx, gy + dy)
 
-    each(gy_count, lambda k: greet(gx, wrap(gy, k, gy_count)))
+    bits = [1 << b for b in range(1, gy_count.bit_length() - 1)] + [1]
+
+    def flip(bit):
+        return gy + bit * (1 - 2 * lax.rem(gy // bit, 2))
+
+    for bit in bits[:-1]:
+        greet(gx, flip(bit))
+    for dy in (-1, 1):
+        @pl.when(inside(0, dy))
+        def _():
+            greet(gx, gy + dy)
+
 
     lane = iota((rows, lanes), 1)
     half = lanes // 2
@@ -124,7 +135,7 @@
     ).astype(BF16)
     l1 = iota((width1, lanes), 0)
     j2 = l1 // 2
-    place = (j2 % 4) * 16 + j2 // 4
+    place = ((j2 + gy) % 4) * 16 + j2 // 4
     down1[...] = jnp.where(
         (l1 < lanes) & (iota((width1, lanes), 1) % half == place), 1.0, 0.0
     ).astype(BF16)
@@ -166,20 +177,21 @@
                 get_strips(source, pl.ds(start, 8, 8)) + get_strips(source, pl.ds(start + 1, 8, 8))
             )
         means = 0.25 * exact_dot(jnp.concatenate(parts, 0), down1[...])
-        low = iota((16, lanes), 1) < half
+        low = (iota((16, lanes), 1) // 16 + 8 - lax.rem(gy, 8)) % 8 < 4
         return jnp.where(low, means[0:16], means[16:32])
 
     def beside_count(at, count):
         return (at + count - 1) // count + 1 - (at + 1) // count
 
     pl.semaphore_wait(
-        barrier, gx_count + gy_count - 2 + beside_count(gx, gx_count) * beside_count(gy, gy_count)
+        barrier,
+        gx_count + len(bits) - 2 + beside_count(gy, gy_count) * (1 + beside_count(gx, gx_count)),
     )
 
-    def tell_row(k):
-        pl.semaphore_signal(row_wave, inc=1, device_id=(wrap(gx, k, gx_count), gy), device_id_type=MESH)
-
-    each(gx_count, tell_row)
+    def tell(n):
+        pl.semaphore_signal(told.at[n], inc=1, device_id=(gx, flip(bits[n])), device_id_type=MESH)
+
+    tell(0)
 
     top, bottom = slice(0, HALO), slice(rows - HALO, rows)
     above, below = slice(ROWS_PAD, base), slice(base + rows, base + rows + HALO)
@@ -285,7 +297,6 @@
     def line_start(turn):
         block_copy(turn, 0, me, partner).start()
         each(gx_count, lambda d: along_line(turn, gx_count - d).start())
-        each(per_row, lambda j: across(turn, 0, per_row - j).start())
 
     def line_pass(turn):
         def pass_line(d):
@@ -322,6 +333,11 @@
     put_strips(r1, slice(base1, base1 + half_rows), 0.25 * exact_dot(own, down0[0:cols, :]))
     rbuf[0, me] = pack_level2(r1)
     line_start(0)
+    for n in range(len(bits)):
+        pl.semaphore_wait(told.at[n], 1)
+        if n < len(bits) - 1:
+            tell(n + 1)
+    each(per_row, lambda j: across(0, 0, per_row - j).start())
     zero_tile = jnp.zeros((ROWS_PAD, width), F32)
     for ref in (vA, vB):
         ref[0:ROWS_PAD, :] = zero_tile
@@ -417,7 +433,6 @@
     sweep_block(aP, bP, gP, wP, 1)
     residual_block(bP, r1, gP, sP, 1, (base1, base1 + half_rows))
     rbuf[1, me] = pack_level2(r1)
-    pl.semaphore_wait(row_wave, gx_count - 1)
     gather_start(1)
     line_pass(0)
 
@@ -428,18 +443,15 @@
             for u in range(gy_count // 8):
                 for tl in range(2):
                     tiles = [rbuf[turn, x * gy_count + u * 8 + g, tl * 8 : tl * 8 + 8, :] for g in range(8)]
+                    tiles = [tiles[-b % 8] for b in range(8)]
                     for bit in (1, 2, 4):
                         keep = (block & bit) == 0
-                        fresh = list(tiles)
-                        for g in range(8):
-                            if g & bit == 0:
-                                lo, hi = tiles[g], tiles[g | bit]
-                                fresh[g] = jnp.where(keep, lo, pltpu.roll(hi, 16 * bit, 1))
-                                fresh[g | bit] = jnp.where(keep, pltpu.roll(lo, lanes - 16 * bit, 1), hi)
-                        tiles = fresh
+                        tiles = [jnp.where(keep, tiles[b], tiles[(b - bit) % 8]) for b in range(8)]
                     for b in range(8):
                         t, r = (b // 4) * 2 + tl, b % 4
-                        target[t * 4 + r, 8 * x : 8 * x + 8, u * lanes : (u + 1) * lanes] = tiles[b]
+                        target[t * 4 + r, 8 * x : 8 * x + 8, u * lanes : (u + 1) * lanes] = pltpu.roll(
+                            tiles[b], (lanes - 16 * b) % lanes, 1
+                        )
 
     lane_q = iota((p_count, q_count), 1)
     rows_q = slice(8, 8 + p_count)
@@ -724,12 +736,16 @@
     v2 = sweep_window(2, [w2w[t] * source2[t] for t in range(4)], source2)
     source3 = halved_window(residual_window(2, v2, source2), 32)
     v3 = sweep_window(3, [w3w[t] * source3[t] for t in range(2)], source3)
-    source4 = halved_window(residual_window(3, v3, source3), 64)[0]
+    left3 = residual_window(3, v3, source3)
+    left3 = 0.25 * (left3[0] + left3[1])
     place = lax.rem(gy, 8) * 16
-    mine = pltpu.roll(source4[4:12], lax.rem(place + lanes - 8, lanes), 1)
-    lane_c = iota((8, lanes), 1)
-    cbuf[me] = jnp.where((lane_c >= place) & (lane_c < place + 16), mine, 0.0)
-
+    turns = lax.rem(place + lanes - 8, lanes), lax.rem(place + lanes + half - 8, lanes)
+    lane_c = iota((4, lanes), 1)
+    upper, lower = (
+        pltpu.roll(left3[at : at + 4], turns[0], 1) + pltpu.roll(left3[at : at + 4], turns[1], 1) for at in (4, 8)
+    )
+    after = (lane_c + lanes - place) % lanes
+    cbuf[me] = jnp.where(after < 16, upper, jnp.where((after >= half) & (after < half + 16), lower, 0.0))
     each(total, coarse_send)
     line_sent(0)
     gather_sent(1)
@@ -745,13 +761,18 @@
     for x in range(gx_count):
         for u in range(gy_count // 8):
             first = x * gy_count + u * 8
-            pairs = [cbuf[first + k] + cbuf[first + k + 1] for k in range(0, 8, 2)]
-            g4[0, x * 8 : x * 8 + 8, u * lanes : (u + 1) * lanes] = (pairs[0] + pairs[1]) + (pairs[2] + pairs[3])
+            left, right = (
+                (cbuf[k] + cbuf[k + 1]) + (cbuf[k + 2] + cbuf[k + 3]) for k in (first, first + 4)
+            )
+            at = slice(u * lanes, (u + 1) * lanes)
+            g4[0, x * 8 : x * 8 + 4, at] = jnp.where(lane_c < half, left, right)
+            g4[0, x * 8 + 4 : x * 8 + 8, at] = pltpu.roll(jnp.where(lane_c < half, right, left), half, 1)
     e = coarse()
     e = e[0, pl.ds(pl.multiple_of(gx * 8, 8), 24), :][4 : 4 + window]
-    e = pltpu.roll(e, lax.rem(q_count + 8 - gy * 16 + q_count, q_count), 1)[:, 0:lanes]
-    e = jnp.where(in_domain(lanes), e, 0.0)
-    e = e + pltpu.roll(e, 64, 1)
+    near_e, far_e = (
+        pltpu.roll(e, lax.rem(2 * q_count + 8 + k - gy * 16, q_count), 1)[:, 0:lanes] for k in (0, half)
+    )
+    e = jnp.where(in_domain(half), jnp.where(lane_w < half, near_e, far_e), 0.0)
     v3 = [v3[t] + e for t in range(2)]
     v3 = sweep_window(3, sweep_window(3, v3, source3), source3)
     e = [v3[t] + pltpu.roll(v3[t], 32, 1) for t in range(2)]
@@ -788,7 +809,7 @@
 
     def body(right_side, shift):
         rows, cols = right_side.shape
-        assert cols == 256 and rows == 128 and gy_count % 8 == 0
+        assert cols == 256 and rows == 128 and gy_count % 8 == 0 and gy_count & (gy_count - 1) == 0
         ext, width = rows + 2 * (HALO + ROWS_PAD), cols + 128
         ext1, width1 = ext // 2 + 2 * ROWS_PAD, 256
         wide1 = rows // 2 + 2 * (ROW_HALO + ROWS_PAD)
@@ -808,13 +829,13 @@
             + [V((rows, 128), F32)] * 2 + [V((ext, 128), F32)] * 2
             + [V((width, width1), BF16), V((width1, width), BF16), V((width1, 128), BF16), V((4 * q, width1), BF16)]
             + [V((width1, 128), BF16), V((128, width1), BF16)]
-            + [V((2, total, 16, 128), F32), V((total, 8, 128), F32)]
+            + [V((2, total, 16, 128), F32), V((total, 4, 128), F32)]
             + levels
             + [V((4, 24, width1), F32)]
             + [V((4, window, 128), F32)] * 2 + [V((2, window, 128), F32)] * 2
             + [V((5, p, q), F32), V((2, p, q), F32), V((20, p + 16, q), F32)]
             + [dma((10,)), dma((10,)), dma((4,)), dma((4,)), dma((2, total)), dma((2, total)), dma((2,))]
-            + [pltpu.SemaphoreType.REGULAR]
+            + [pltpu.SemaphoreType.REGULAR((gy_count.bit_length() - 1,))]
         )
         out = pltpu.VMEM((2,) + right_side.shape, F32)
         both = pl.pallas_call(

time: 32 us -> 31.2 us (0.975)
  Pallas kernels: 30.5 us -> 29.7 us
    pallas_call x1, Pallas kernels: 30.5 us -> 29.7 us  [body(): pl.pallas_call(functools.partial(kernel, gx_count, gy_count), out_shape=o...]
where the time goes in v4:
time: 31.2 us; the launch traced here: 31 us
  Pallas kernels  29.7 us (95%)
  local copies, waits for them, and re-layouts  0.72 us (2%)
  between operations  0.64 us (2%)
    pallas_call x1, Pallas kernels, body(): pl.pallas_call(functools.partial(kernel, gx_count, gy_count), out_shape=o...  29.7 us
    squeeze x1, local copies, waits for them, and re-layouts, body(): return (both[0], both[1])  0.72 us

profile of v4, /device:TPU:0, one launch (start us, length us, event | category | flops | bytes accessed | tf_op | source)
XLA Modules:
  0.0 31.0 jit_solution(13352150531353975030)
XLA Ops:
  0.6 29.7 %shard_map.41 = f32[2,128,256]{2,1,0:T(8,128)S(1)} custom-call(f32[128,256]{1,0:T(8,128)} %g_hbm.1, f32[128,256]{1,0:T(8,128)} %s_hbm.1), custom_call_target="tpu_custom_call" | custom-call | tf_op jit(solution)/shard_map/pallas_call | solution.py:841
  30.3 0.7 %slice_bitcast_fusion = (f32[128,256]{1,0:T(8,128)}, f32[128,256]{1,0:T(8,128)}) fusion(f32[2,128,256]{2,1,0:T(8,128)S(1)} %shard_map.41), kind=kLoop, calls=%fused_computation | loop fusion | bytes 524288 | tf_op jit(solution)/shard_map/squeeze | solution.py:851

commit v5 on v4

--- a/solution.py
+++ b/solution.py
@@ -226,6 +226,10 @@
     partner = (gx, gy + 1 - 2 * core)
 
     def zigzag(j, count):
+        if total <= 64:
+            width_of = count // gx_count
+            lines = [0] + sorted(range(1, gx_count), key=lambda d: -abs(2 * d - gx_count))
+            return lines[j // width_of] * width_of + j % width_of
         odd = j % 2
         return odd * ((j + 1) // 2) + (1 - odd) * (count - j // 2)
 
@@ -781,8 +785,9 @@
     raised = exact_dot(jnp.concatenate(v2, 0), up_w[...])
     for t in range(4):
         put_window(t, raised[t * window : (t + 1) * window])
-    b1[wide1, :] = b1[wide1, :] + get_strips(r1, wide1)
     near_w = (base_w - 8, base_w + half_rows + 8)
+    around_w = slice(near_w[0] - 8, near_w[1] + 8)
+    b1[around_w, :] = b1[around_w, :] + get_strips(r1, around_w)
     sweep_block(b1, a1, g1, w1, 1, near_w)
     sweep_block(a1, b1, g1, w1, 1, near_w)
     raised = exact_dot(b1[slice(*near_w), :], up0[...])

time: 31.2 us -> 30.8 us (0.987)
  Pallas kernels: 29.7 us -> 29.3 us
    pallas_call x1, Pallas kernels: 29.7 us -> 29.3 us  [body(): pl.pallas_call(functools.partial(kernel, gx_count, gy_count), out_shape=o...]
where the time goes in v5:
time: 30.8 us; the launch traced here: 30.7 us
  Pallas kernels  29.3 us (95%)
  local copies, waits for them, and re-layouts  0.72 us (2%)
  between operations  0.64 us (2%)
    pallas_call x1, Pallas kernels, body(): pl.pallas_call(functools.partial(kernel, gx_count, gy_count), out_shape=o...  29.3 us
    squeeze x1, local copies, waits for them, and re-layouts, body(): return (both[0], both[1])  0.72 us

profile of v5, /device:TPU:0, one launch (start us, length us, event | category | flops | bytes accessed | tf_op | source)
XLA Modules:
  0.0 30.7 jit_solution(8276652711599468001)
XLA Ops:
  0.6 29.3 %shard_map.41 = f32[2,128,256]{2,1,0:T(8,128)S(1)} custom-call(f32[128,256]{1,0:T(8,128)} %g_hbm.1, f32[128,256]{1,0:T(8,128)} %s_hbm.1), custom_call_target="tpu_custom_call" | custom-call | tf_op jit(solution)/shard_map/pallas_call | solution.py:846
  30.0 0.7 %slice_bitcast_fusion = (f32[128,256]{1,0:T(8,128)}, f32[128,256]{1,0:T(8,128)}) fusion(f32[2,128,256]{2,1,0:T(8,128)S(1)} %shard_map.41), kind=kLoop, calls=%fused_computation | loop fusion | bytes 524288 | tf_op jit(solution)/shard_map/squeeze | solution.py:856

commit v6 on v5

--- a/solution.py
+++ b/solution.py
@@ -735,7 +735,7 @@
     sweep_block(a1, b1, g1, w1, 1)
     sweep_block(b1, a1, g1, w1, 1)
     sweep_block(a1, b1, g1, w1, 1)
-    residual_block(b1, r1, g1, s1, 1)
+    residual_block(b1, r1, g1, s1, 1, (base_w - 24, base_w + half_rows + 24))
     source2 = pack_window(r1)
     v2 = sweep_window(2, [w2w[t] * source2[t] for t in range(4)], source2)
     source3 = halved_window(residual_window(2, v2, source2), 32)

time: 30.8 us -> 30.8 us (level)
  no operation moved by 1% of the time
where the time goes in v6:
time: 30.8 us; the launch traced here: 30.7 us
  Pallas kernels  29.3 us (95%)
  local copies, waits for them, and re-layouts  0.72 us (2%)
  between operations  0.64 us (2%)
    pallas_call x1, Pallas kernels, body(): pl.pallas_call(functools.partial(kernel, gx_count, gy_count), out_shape=o...  29.3 us
    squeeze x1, local copies, waits for them, and re-layouts, body(): return (both[0], both[1])  0.72 us

profile of v6, /device:TPU:0, one launch (start us, length us, event | category | flops | bytes accessed | tf_op | source)
XLA Modules:
  0.0 30.7 jit_solution(17850580647019655118)
XLA Ops:
  0.6 29.3 %shard_map.41 = f32[2,128,256]{2,1,0:T(8,128)S(1)} custom-call(f32[128,256]{1,0:T(8,128)} %g_hbm.1, f32[128,256]{1,0:T(8,128)} %s_hbm.1), custom_call_target="tpu_custom_call" | custom-call | tf_op jit(solution)/shard_map/pallas_call | solution.py:846
  30.0 0.7 %slice_bitcast_fusion = (f32[128,256]{1,0:T(8,128)}, f32[128,256]{1,0:T(8,128)}) fusion(f32[2,128,256]{2,1,0:T(8,128)S(1)} %shard_map.41), kind=kLoop, calls=%fused_computation | loop fusion | bytes 524288 | tf_op jit(solution)/shard_map/squeeze | solution.py:856
